TPU v7x, 256 devices: a whole 4x4x8 slice. The times are simulated.
256 devices in a mesh: rep: 16 (over x, z_hi, core), stripe: 16 (over y, z_lo).
Axes of the slice: x: 4, y: 4, z: 8 (z_hi: 2, z_lo: 4; z = z_hi * 4 + z_lo), core: 2. Of those that a mesh axis runs over, the one named last changes fastest.
Arguments:
- activations: bfloat16 [4096, 4096], P('rep'), may hold values from -6 to 6
- out_grads: bfloat16 [4096, 8192], P('rep', 'stripe'), may hold values from -4 to 4
- statistics: float32 [16, 16, 512, 512], P('rep', 'stripe'), may hold values from -48 to 4608, as said below
- owner_blocks: int32 [16, 8], P('stripe'), may hold values from 0 to 7, each once within a row
Outputs:
- preconditioned: float32 [4096, 8192], P(None, 'stripe')
- new_stats: float32 [16, 16, 512, 512], P('rep', 'stripe')
Inputs may be any that keep to these rules, and one draw needn't show every extreme that they name: statistics[p, s] is symmetric positive definite for every p and s. `owner_blocks`: each row lists every row block 0 to 7 exactly once.
All inputs are finite; a program needn't handle non-finite values.
Results may differ from a plain program's by a relative error of at most 0.0003.
Values sent between devices are 32-bit elements; how exact they have to be, the bound alone decides.
A program may use at most 128 MiB of HBM per device.

v0:
```python
import jax
import jax.numpy as jnp
from jax import lax
from jax.sharding import Mesh
from jax.sharding import PartitionSpec as P

BLOCK = 512
ITERS = 2
REP = ("rep_0", "rep_1", "rep_2")
REP_STRIPE = ("rep_0", "rep_1", "rep_2", "stripe_0", "stripe_1")
STRIPE = ("stripe_0", "stripe_1")
decay_rate = 0.95
damping = 0.25
epsilon = 1e-06
highest = lax.Precision.HIGHEST


def partner(shard, axis, stride):
    return lax.ppermute(shard, axis, [(i, i ^ 1 << stride) for i in range(lax.axis_size(axis))])


def by_axis(shard, axes):
    for axis in axes:
        shard = lax.psum(shard, axis)
    return shard


def inverse_root(damped):
    identity = jnp.eye(damped.shape[-1], dtype=damped.dtype)
    frob_norm = jnp.sqrt(jnp.sum(damped * damped, axis=(-2, -1), keepdims=True) + epsilon)
    scaled = damped / frob_norm
    root_now = identity * frob_norm ** (-0.25)
    for sweep in range(ITERS):
        factor = (5.0 * identity - scaled) * 0.25
        root_now = jnp.matmul(root_now, factor, precision=highest)
        if sweep + 1 < ITERS:
            square = jnp.matmul(factor, factor, precision=highest)
            fourth = jnp.matmul(square, square, precision=highest)
            scaled = jnp.matmul(fourth, scaled, precision=highest)
    return root_now


def slot_terms(activations, out_grads, blocks_of, pair_count, piece_rows, row_count):
    tokens_here, in_width = activations.shape
    per_block = BLOCK // piece_rows
    shaped = activations.reshape(tokens_here, in_width // piece_rows, piece_rows)
    slot_count = row_count // piece_rows
    slot_ids = jnp.arange(slot_count, dtype=jnp.int32)
    block_ids = jnp.take(blocks_of, slot_ids % pair_count)
    half_ids = slot_ids // pair_count % per_block
    chosen = jnp.take(shaped, block_ids * per_block + half_ids, axis=1)
    products = jnp.einsum("tkp,tc->kpc", chosen, out_grads, preferred_element_type=jnp.float32)
    return products.reshape(slot_count * piece_rows, out_grads.shape[1])


def per_device(activations, out_grads, statistics, owner_blocks):
    rep_count = lax.axis_size(REP)
    pair_count = rep_count // 2
    pair_bit = rep_count.bit_length() - 2
    half_rows = BLOCK // 2
    my_index = lax.axis_index(REP)
    is_left = my_index < pair_count
    blocks_of = owner_blocks[0]
    own_half = lax.psum_scatter(
        slot_terms(
            activations, out_grads, blocks_of, pair_count, half_rows, half_rows * lax.axis_size(REP)
        ),
        REP,
        scatter_dimension=0,
        tiled=True,
    )
    partner_half = partner(own_half, REP, pair_bit)
    gradient = jnp.where(
        is_left,
        jnp.concatenate([own_half, partner_half], axis=0),
        jnp.concatenate([partner_half, own_half], axis=0),
    )
    facing = jnp.where(is_left, gradient, gradient.T)
    new_stat = decay_rate * statistics[0, 0] + jnp.dot(facing, facing.T, precision=highest)
    trace_sum = by_axis(jnp.trace(new_stat), REP_STRIPE)
    mean_diag = trace_sum / (rep_count * lax.axis_size(STRIPE) * BLOCK)
    identity = jnp.eye(BLOCK, dtype=jnp.float32)
    root_now = inverse_root(new_stat + damping * mean_diag * identity)
    partner_root = partner(root_now, REP, pair_bit)
    left_root = jnp.where(is_left, root_now, partner_root)
    right_root = jnp.where(is_left, partner_root, root_now)
    row_start = jnp.where(is_left, 0, half_rows).astype(jnp.int32)
    my_rows = lax.dynamic_slice_in_dim(left_root, row_start, half_rows, 0)
    grad_rows = lax.dynamic_slice_in_dim(gradient, row_start, half_rows, 0)
    precond_half = jnp.dot(
        jnp.dot(my_rows, gradient, precision=highest), right_root, precision=highest
    )
    grad_sq, prec_sq = (
        by_axis(jnp.sum(grad_rows * grad_rows), REP_STRIPE),
        by_axis(jnp.sum(precond_half * precond_half), REP_STRIPE),
    )
    scaled = precond_half * jnp.sqrt(grad_sq / (prec_sq + epsilon))
    gathered = lax.all_gather(scaled[None], REP, axis=0, tiled=True)
    pair_ids = jnp.arange(pair_count, dtype=jnp.int32)
    inverse = jnp.sum(
        pair_ids[:, None] * (blocks_of[:, None] == pair_ids[None, :]).astype(jnp.int32), axis=0
    )
    row_order = jnp.stack([inverse, inverse + pair_count], axis=1).reshape(-1)
    preconditioned = jnp.take(gathered, row_order, axis=0).reshape(
        pair_count * BLOCK, gathered.shape[2]
    )
    return (preconditioned, new_stat[None, None])


def solution(mesh):
    split = Mesh(
        mesh.devices.reshape(4, 2, 2, 4, 4), ("rep_0", "rep_1", "rep_2", "stripe_0", "stripe_1")
    )
    return jax.shard_map(
        per_device,
        mesh=split,
        in_specs=(P(REP, None), P(REP, STRIPE), P(REP, STRIPE, None, None), P(STRIPE, None)),
        out_specs=(P(None, STRIPE), P(REP, STRIPE, None, None)),
        check_vma=False,
    )
```

profile of v0, /device:TPU:1, one launch (start us, length us, event | category | flops | bytes accessed | tf_op | source)
XLA Modules:
  0.0 449.1 jit_solution(16025409931431591571)
XLA Ops:
  7.2 0.0 copy-start
  7.2 0.0 reduce-scatter.2.cloned.1.call-start
  7.2 0.8 select_reduce_fusion.1
  8.0 0.1 copy.25
  8.1 0.1 reshape.203
  8.2 1.3 gather_fusion
  9.6 4.1 copy.26
  13.7 2.8 copy.27
  16.5 2.0 gather_fusion.1
  18.5 6.7 %fusion = f32[16,256,512]{2,1,0:T(8,128)} fusion(bf16[16,256,256]{2,1,0:T(8,128)(2,1)} %gather_fusion.1, pred[16]{0:T(512)(128)(4,1)S(1)} %get-tuple-element.16, bf16[256,512]{1,0:T(8,128)(2,1)S(1)} %copy-done), kind=kOutput, calls=%fused_computation.4 | convolution fusion | flops 1074790400 | bytes 10747920 | tf_op jit(solution)/shard_map/tkp,tc->kpc/dot_general | solution.py:52
  25.2 8.9 %copy.29 = f32[4096,512]{0,1:T(8,128)} copy(f32[4096,512]{1,0:T(8,128)} %bitcast.40) | data formatting | bytes 16777216 | tf_op jit(solution)/shard_map/reshape | solution.py:53
  34.1 0.0 reduce-scatter.2.cloned.1.call-update
  34.2 0.0 all-gather.3.cloned.1.call-start
  34.2 142.1 %reduce-scatter.2.cloned.1.call-done = f32[256,512]{0,1:T(8,128)} async-done(((f32[4096,512]{0,1:T(8,128)}), f32[256,512]{0,1:T(8,128)}) %reduce-scatter.2.cloned.1.call-update) | async-done | bytes 524304 | tf_op jit(solution)/shard_map/reduce_scatter | solution.py:64
  176.3 1.2 collective-permute-start
  177.5 11.7 %collective-permute-done = f32[256,512]{0,1:T(8,128)S(1)} collective-permute-done((f32[256,512]{0,1:T(8,128)}, f32[256,512]{0,1:T(8,128)S(1)}, u32[]{:S(2)}, u32[]{:S(2)}) %collective-permute-start) | collective-permute-done | bytes 524320 | tf_op jit(solution)/shard_map/ppermute | solution.py:19
  189.3 1.6 maximum_select_fusion
  190.9 0.3 copy.31
  191.2 5.6 %select_reduce_fusion = (f32[]{:T(128)}, f32[512,512]{1,0:T(8,128)S(1)}) fusion(f32[512,512]{1,0:T(8,128)S(1)} %copy.31, pred[]{:T(512)S(6)} %lt.75, f32[256,512]{0,1:T(8,128)} %reduce-scatter.2.cloned.1.call-done, f32[256,512]{0,1:T(8,128)} %copy-done.3, f32[1,1,512,512]{3,2,1,0:T(8,128)} %param.6), kind=kOutput, calls=%fused_computation.22 | convolution fusion | flops 1612972032 | bytes 4194309 | tf_op jit(solution)/shard_map/dot_general | solution.py:79
  196.8 6.6 %psum.105 = f32[]{:T(128)} all-reduce(f32[]{:T(128)} %get-tuple-element.12), channel_id=1, replica_groups=mesh['rep_0'=4,'rep_1'=2,'rep_2'=2,'stripe_0'=4,'stripe_1'=4] {'rep_0'}, use_global_device_ids=true, to_apply=%region_3.4 | all-reduce | flops 1 | bytes 8 | tf_op jit(solution)/shard_map/psum | solution.py:24
  203.4 8.3 %psum.106 = f32[]{:T(128)} all-reduce(f32[]{:T(128)} %psum.105), channel_id=1, replica_groups=mesh['rep_0'=4,'rep_1'=2,'rep_2'=2,'stripe_0'=4,'stripe_1'=4] {'rep_1'}, use_global_device_ids=true, to_apply=%region_4.5 | all-reduce | flops 1 | bytes 8 | tf_op jit(solution)/shard_map/psum | solution.py:24
  211.6 9.8 %psum.107 = f32[]{:T(128)} all-reduce(f32[]{:T(128)} %psum.106), channel_id=1, replica_groups=mesh['rep_0'=4,'rep_1'=2,'rep_2'=2,'stripe_0'=4,'stripe_1'=4] {'rep_2'}, use_global_device_ids=true, to_apply=%region_5.6 | all-reduce | flops 1 | bytes 8 | tf_op jit(solution)/shard_map/psum | solution.py:24
  221.4 7.5 %psum.108 = f32[]{:T(128)} all-reduce(f32[]{:T(128)} %psum.107), channel_id=1, replica_groups=mesh['rep_0'=4,'rep_1'=2,'rep_2'=2,'stripe_0'=4,'stripe_1'=4] {'stripe_0'}, use_global_device_ids=true, to_apply=%region_6.7 | all-reduce | flops 1 | bytes 8 | tf_op jit(solution)/shard_map/psum | solution.py:24
  228.9 10.8 %psum.109 = f32[]{:T(128)} all-reduce(f32[]{:T(128)} %psum.108), channel_id=1, replica_groups=mesh['rep_0'=4,'rep_1'=2,'rep_2'=2,'stripe_0'=4,'stripe_1'=4] {'stripe_1'}, use_global_device_ids=true, to_apply=%region_7.8 | all-reduce | flops 1 | bytes 8 | tf_op jit(solution)/shard_map/psum | solution.py:24
  240.3 1.0 multiply_reduce_fusion
  242.0 2.0 fusion.12
  244.0 0.0 copy-start.2
  244.0 1.8 fusion.46
  245.8 1.9 fusion.4
  247.8 3.1 fusion.9
  250.9 1.8 fusion.47
  252.8 0.7 collective-permute-start.1
  253.4 0.7 multiply_reduce_fusion.2
  254.2 20.9 %collective-permute-done.1 = f32[512,512]{1,0:T(8,128)S(1)} collective-permute-done((f32[512,512]{1,0:T(8,128)S(1)}, f32[512,512]{1,0:T(8,128)S(1)}, u32[]{:S(2)}, u32[]{:S(2)}) %collective-permute-start.1) | collective-permute-done | bytes 1048608 | tf_op jit(solution)/shard_map/ppermute | solution.py:19
  275.0 2.7 fusion.15
  277.8 1.8 multiply_reduce_fusion.1
  279.5 6.6 %all-reduce.2 = (f32[]{:T(128)}, f32[]{:T(128)}) all-reduce(f32[]{:T(128)} %multiply_reduce_fusion.2, f32[]{:T(128)} %get-tuple-element.14), channel_id=1, replica_groups=mesh['rep_0'=4,'rep_1'=2,'rep_2'=2,'stripe_0'=4,'stripe_1'=4] {'rep_0'}, use_global_device_ids=true, to_apply=%region_10.11 | all-reduce | flops 2 | bytes 16 | tf_op jit(solution)/shard_map/psum | solution.py:24
  286.1 8.4 %all-reduce.4 = (f32[]{:T(128)}, f32[]{:T(128)}) all-reduce(f32[]{:T(128)} %get-tuple-element.6, f32[]{:T(128)} %get-tuple-element.7), channel_id=1, replica_groups=mesh['rep_0'=4,'rep_1'=2,'rep_2'=2,'stripe_0'=4,'stripe_1'=4] {'rep_1'}, use_global_device_ids=true, to_apply=%region_11.12 | all-reduce | flops 2 | bytes 16 | tf_op jit(solution)/shard_map/psum | solution.py:24
  294.5 10.6 %all-reduce.3 = (f32[]{:T(128)}, f32[]{:T(128)}) all-reduce(f32[]{:T(128)} %get-tuple-element.10, f32[]{:T(128)} %get-tuple-element.11), channel_id=1, replica_groups=mesh['rep_0'=4,'rep_1'=2,'rep_2'=2,'stripe_0'=4,'stripe_1'=4] {'rep_2'}, use_global_device_ids=true, to_apply=%region_12.13 | all-reduce | flops 2 | bytes 16 | tf_op jit(solution)/shard_map/psum | solution.py:24
  305.1 6.8 %all-reduce.1 = (f32[]{:T(128)}, f32[]{:T(128)}) all-reduce(f32[]{:T(128)} %get-tuple-element.8, f32[]{:T(128)} %get-tuple-element.9), channel_id=1, replica_groups=mesh['rep_0'=4,'rep_1'=2,'rep_2'=2,'stripe_0'=4,'stripe_1'=4] {'stripe_0'}, use_global_device_ids=true, to_apply=%region_13.14 | all-reduce | flops 2 | bytes 16 | tf_op jit(solution)/shard_map/psum | solution.py:24
  311.8 7.2 %all-reduce = (f32[]{:T(128)}, f32[]{:T(128)}) all-reduce(f32[]{:T(128)} %get-tuple-element.4, f32[]{:T(128)} %get-tuple-element.5), channel_id=1, replica_groups=mesh['rep_0'=4,'rep_1'=2,'rep_2'=2,'stripe_0'=4,'stripe_1'=4] {'stripe_1'}, use_global_device_ids=true, to_apply=%region_14.15 | all-reduce | flops 2 | bytes 16 | tf_op jit(solution)/shard_map/psum | solution.py:24
  320.3 0.8 broadcast_multiply_fusion
  321.2 0.0 all-gather.3.cloned.1.call-update
  321.2 0.1 reshape.206
  321.3 0.1 broadcast_in_dim.39
  321.4 107.2 %all-gather.3.cloned.1.call-done = f32[4096,512]{1,0:T(8,128)} async-done(((f32[256,512]{1,0:T(8,128)}), f32[4096,512]{1,0:T(8,128)}) %all-gather.3.cloned.1.call-update) | async-done | bytes 8388624 | tf_op jit(solution)/shard_map/all_gather | solution.py:98
  428.6 7.7 %gather_fusion.2 = f32[16,256,512]{2,1,0:T(8,128)} fusion(f32[16,256,512]{2,1,0:T(8,128)} %bitcast.41, s32[1024]{0:T(1024)S(1)} %pad_clamp_fusion), kind=kCustom, calls=%fused_computation.2 | custom fusion | bytes 16777280 | tf_op jit(solution)/shard_map/jit(_take)/gather | solution.py:104
  436.3 6.0 %bitcast_select_fusion = f32[4096,512]{1,0:T(8,128)} fusion(f32[16,256,512]{2,1,0:T(8,128)} %gather_fusion.2, pred[4096]{0:T(1024)(128)(4,1)S(1)} %broadcast_in_dim.40), kind=kLoop, calls=%fused_computation.3 | loop fusion | flops 2097152 | bytes 16781312 | tf_op jit(solution)/shard_map/jit(_take)/select_n | solution.py:104
  (16 shorter events, 0.1 us)
Async XLA Ops:
  7.2 11.4 %copy-start = (bf16[256,512]{1,0:T(8,128)(2,1)S(1)}, bf16[256,512]{1,0:T(8,128)(2,1)}, u32[]{:S(2)}) copy-start(bf16[256,512]{1,0:T(8,128)(2,1)} %param.5) | copy-start | bytes 786436
  7.2 169.2 %reduce-scatter.2.cloned.1.call-start = ((), (), s32[]{:S(2)}) async-start(), calls=%async_computation.1 | async-start | bytes 8912896 | tf_op jit(solution)/shard_map/reduce_scatter | solution.py:64
  34.2 394.5 %all-gather.3.cloned.1.call-start = ((), (), s32[]{:S(2)}) async-start(), calls=%async_computation.2 | async-start | bytes 8912896 | tf_op jit(solution)/shard_map/all_gather | solution.py:98
  176.3 12.9 %collective-permute-start = (f32[256,512]{0,1:T(8,128)}, f32[256,512]{0,1:T(8,128)S(1)}, u32[]{:S(2)}, u32[]{:S(2)}) collective-permute-start(f32[256,512]{0,1:T(8,128)} %reduce-scatter.2.cloned.1.call-done), channel_id=1, source_target_pairs={{0,128},{16,144},{32,160},{48,176},{64,192},{80,208},{96,224},{112... | collective-permute-start | bytes 1572872 | tf_op jit(solution)/shard_map/ppermute | solution.py:19
  189.3 1.6 copy-start.3
  196.8 45.2 %copy-start.1 = (f32[512,512]{1,0:T(8,128)}, f32[512,512]{1,0:T(8,128)S(1)}, u32[]{:S(2)}) copy-start(f32[512,512]{1,0:T(8,128)S(1)} %get-tuple-element.13) | copy-start | bytes 3145732
  244.0 1.9 copy-start.2
  252.8 22.3 %collective-permute-start.1 = (f32[512,512]{1,0:T(8,128)S(1)}, f32[512,512]{1,0:T(8,128)S(1)}, u32[]{:S(2)}, u32[]{:S(2)}) collective-permute-start(f32[512,512]{1,0:T(8,128)S(1)} %fusion.47), channel_id=1, source_target_pairs={{0,128},{16,144},{32,160},{48,176},{64,192},{80,208},{96,224},{112... | collective-permute-start | bytes 3145736 | tf_op jit(solution)/shard_map/ppermute | solution.py:19
Sparse Core Ops, SparseCore 0:
  34.3 142.0 reduce-scatter.1
  321.3 107.2 all-gather.2
where the time goes:
time: 450 us; the launch traced here: 449 us
  waiting for transfers between devices  282 us (63%)
  blocking collectives  82.5 us (18%)
  local copies, waits for them, and re-layouts  27.6 us (6%)
  matrix products  27.4 us (6%)
  between operations  16.8 us (4%)
  other arithmetic  10.9 us (2%)
    reduce_scatter x1, waiting for transfers between devices, per_device(): lax.psum_scatter(slot_terms(activations, out_grads, blocks_of, pair_count...  142 us
    all_gather x1, waiting for transfers between devices, per_device(): gathered = lax.all_gather(scaled[None], REP, axis=0, tiled=True)  107 us
    psum x10, blocking collectives, by_axis(): shard = lax.psum(shard, axis)  82.5 us
    ppermute x2, waiting for transfers between devices, partner(): lax.ppermute(shard, axis, [(i, i ^ 1 << stride) for i in range(lax.axis_s...  32.6 us
  transfers between devices with their start and end apart: 4, of which 4 were waited for; matrix products, arithmetic and copies ran while one was open for 0% of the time, Pallas kernels for 0%

commit v1 on v0

--- a/solution.py
+++ b/solution.py
@@ -21,7 +21,8 @@
 
 def by_axis(shard, axes):
     for axis in axes:
-        shard = lax.psum(shard, axis)
+        parts = lax.all_gather(shard, axis, axis=0, tiled=False)
+        shard = parts.sum(axis=0)
     return shard
 
 

time: 450 us -> 475 us (1.056)
  local copies, waits for them, and re-layouts: 27.6 us -> 51.4 us
  other arithmetic: 10.9 us -> 20 us
  blocking collectives: 82.5 us -> 76 us
    psum x10 -> x0, blocking collectives: 82.5 us -> none  [by_axis(): shard = lax.psum(shard, axis)]
    unnamed x0 -> x10, blocking collectives: none -> 76 us
    unnamed x9 -> x54, local copies, waits for them, and re-layouts: 4.1 us -> 27.9 us
    reduce_sum x0 -> x15, other arithmetic: none -> 9.17 us  [by_axis(): shard = parts.sum(axis=0)]
  transfers between devices with their start and end apart: 4 -> 4, of which waited for: 4 -> 4; matrix products, arithmetic and copies ran while one was open for 0% -> 1% of each run, Pallas kernels for 0% -> 0%
where the time goes in v1:
time: 475 us; the launch traced here: 474 us
  waiting for transfers between devices  280 us (59%)
  blocking collectives  76 us (16%)
  local copies, waits for them, and re-layouts  51.4 us (11%)
  matrix products  27.3 us (6%)
  other arithmetic  20 us (4%)
  between operations  17 us (4%)
    reduce_scatter x1, waiting for transfers between devices, per_device(): lax.psum_scatter(slot_terms(activations, out_grads, blocks_of, pair_count...  142 us
    all_gather x1, waiting for transfers between devices, per_device(): gathered = lax.all_gather(scaled[None], REP, axis=0, tiled=True)  107 us
    unnamed x10, blocking collectives  76 us
    ppermute x2, waiting for transfers between devices, partner(): lax.ppermute(shard, axis, [(i, i ^ 1 << stride) for i in range(lax.axis_s...  30.5 us
    unnamed x54, local copies, waits for them, and re-layouts  27.9 us
  transfers between devices with their start and end apart: 4, of which 4 were waited for; matrix products, arithmetic and copies ran while one was open for 1% of the time, Pallas kernels for 0%

profile of v1, /device:TPU:1, one launch (start us, length us, event | category | flops | bytes accessed | tf_op | source)
XLA Modules:
  0.0 473.6 jit_solution(12012377691681909627)
XLA Ops:
  8.2 1.3 gather_fusion
  9.6 4.1 copy.26
  13.7 2.8 copy.27
  16.5 2.0 gather_fusion.1
  18.5 6.7 %fusion = f32[16,256,512]{2,1,0:T(8,128)} fusion(bf16[16,256,256]{2,1,0:T(8,128)(2,1)} %gather_fusion.1, pred[16]{0:T(512)(128)(4,1)S(1)} %get-tuple-element.16, bf16[256,512]{1,0:T(8,128)(2,1)S(1)} %copy-done), kind=kOutput, calls=%fused_computation.4 | convolution fusion | flops 1074790400 | bytes 10747920 | tf_op jit(solution)/shard_map/tkp,tc->kpc/dot_general | solution.py:53
  25.2 8.9 %copy.29 = f32[4096,512]{0,1:T(8,128)} copy(f32[4096,512]{1,0:T(8,128)} %bitcast.60) | data formatting | bytes 16777216 | tf_op jit(solution)/shard_map/reshape | solution.py:54
  34.2 142.1 %reduce-scatter.2.cloned.1.call-done = f32[256,512]{0,1:T(8,128)} async-done(((f32[4096,512]{0,1:T(8,128)}), f32[256,512]{0,1:T(8,128)}) %reduce-scatter.2.cloned.1.call-update) | async-done | bytes 524304 | tf_op jit(solution)/shard_map/reduce_scatter | solution.py:65
  176.3 1.2 collective-permute-start
  178.2 11.1 %collective-permute-done = f32[256,512]{0,1:T(8,128)S(1)} collective-permute-done((f32[256,512]{0,1:T(8,128)}, f32[256,512]{0,1:T(8,128)S(1)}, u32[]{:S(2)}, u32[]{:S(2)}) %collective-permute-start) | collective-permute-done | bytes 524320 | tf_op jit(solution)/shard_map/ppermute | solution.py:19
  189.3 1.6 maximum_select_fusion
  191.3 5.5 %select_reduce_fusion = (f32[]{:T(128)}, f32[512,512]{1,0:T(8,128)S(1)}) fusion(f32[512,512]{1,0:T(8,128)S(1)} %copy.31, pred[]{:T(512)S(6)} %lt.75, f32[256,512]{0,1:T(8,128)} %reduce-scatter.2.cloned.1.call-done, f32[256,512]{0,1:T(8,128)} %copy-done.3, f32[1,1,512,512]{3,2,1,0:T(8,128)} %param.6), kind=kOutput, calls=%fused_computation.22 | convolution fusion | flops 1612972032 | bytes 4194309 | tf_op jit(solution)/shard_map/dot_general | solution.py:80
  196.7 1.4 dynamic-update-slice
  198.7 6.0 %all-reduce = f32[4]{0:T(128)S(1)} all-reduce(f32[4]{0:T(128)S(1)} %dynamic-update-slice), channel_id=1, replica_groups=mesh['rep_0'=4,'rep_1'=2,'rep_2'=2,'stripe_0'=4,'stripe_1'=4] {'rep_0'}, use_global_device_ids=true, to_apply=%add | all-reduce | flops 4 | bytes 32
  205.3 1.3 dynamic-update-slice.1
  207.2 7.7 %all-reduce.1 = f32[2]{0:T(128)S(1)} all-reduce(f32[2]{0:T(128)S(1)} %dynamic-update-slice.1), channel_id=1, replica_groups=mesh['rep_0'=4,'rep_1'=2,'rep_2'=2,'stripe_0'=4,'stripe_1'=4] {'rep_1'}, use_global_device_ids=true, to_apply=%add.1 | all-reduce | flops 2 | bytes 16
  215.5 1.4 dynamic-update-slice.2
  217.5 9.1 %all-reduce.2 = f32[2]{0:T(128)S(1)} all-reduce(f32[2]{0:T(128)S(1)} %dynamic-update-slice.2), channel_id=1, replica_groups=mesh['rep_0'=4,'rep_1'=2,'rep_2'=2,'stripe_0'=4,'stripe_1'=4] {'rep_2'}, use_global_device_ids=true, to_apply=%add.2 | all-reduce | flops 2 | bytes 16
  227.3 1.3 dynamic-update-slice.3
  229.3 6.9 %all-reduce.3 = f32[4]{0:T(128)S(1)} all-reduce(f32[4]{0:T(128)S(1)} %dynamic-update-slice.3), channel_id=1, replica_groups=mesh['rep_0'=4,'rep_1'=2,'rep_2'=2,'stripe_0'=4,'stripe_1'=4] {'stripe_0'}, use_global_device_ids=true, to_apply=%add.3 | all-reduce | flops 4 | bytes 32
  236.8 1.3 dynamic-update-slice.4
  238.1 10.1 %all-reduce.4 = f32[4]{0:T(128)S(1)} all-reduce(f32[4]{0:T(128)S(1)} %dynamic-update-slice.4), channel_id=1, replica_groups=mesh['rep_0'=4,'rep_1'=2,'rep_2'=2,'stripe_0'=4,'stripe_1'=4] {'stripe_1'}, use_global_device_ids=true, to_apply=%add.4 | all-reduce | flops 4 | bytes 32
  249.5 0.9 multiply_reduce_fusion
  251.0 2.0 fusion.12
  253.0 1.8 fusion.46
  254.9 1.9 fusion.4
  256.9 3.1 fusion.9
  260.0 1.8 fusion.47
  263.3 1.4 dynamic-update-slice.5
  264.7 19.4 %collective-permute-done.1 = f32[512,512]{1,0:T(8,128)S(1)} collective-permute-done((f32[512,512]{1,0:T(8,128)S(1)}, f32[512,512]{1,0:T(8,128)S(1)}, u32[]{:S(2)}, u32[]{:S(2)}) %collective-permute-start.1) | collective-permute-done | bytes 1048608 | tf_op jit(solution)/shard_map/ppermute | solution.py:19
  284.1 2.7 fusion.15
  286.8 1.8 multiply_reduce_fusion.1
  288.6 1.4 dynamic-update-slice.10
  290.0 6.0 %all-reduce.17 = (f32[4]{0:T(128)S(1)}, f32[4]{0:T(128)S(1)}) all-reduce(f32[4]{0:T(128)S(1)} %dynamic-update-slice.5, f32[4]{0:T(128)S(1)} %dynamic-update-slice.10), channel_id=1, replica_groups=mesh['rep_0'=4,'rep_1'=2,'rep_2'=2,'stripe_0'=4,'stripe_1'=4] {'rep_0'}, use_global_device_ids=true, to_apply=%add.5 | all-reduce | flops 8 | bytes 64
  296.6 1.5 dynamic-update-slice.11
  298.8 1.3 dynamic-update-slice.6
  300.1 7.7 %all-reduce.19 = (f32[2]{0:T(128)S(1)}, f32[2]{0:T(128)S(1)}) all-reduce(f32[2]{0:T(128)S(1)} %dynamic-update-slice.6, f32[2]{0:T(128)S(1)} %dynamic-update-slice.11), channel_id=1, replica_groups=mesh['rep_0'=4,'rep_1'=2,'rep_2'=2,'stripe_0'=4,'stripe_1'=4] {'rep_1'}, use_global_device_ids=true, to_apply=%add.6 | all-reduce | flops 4 | bytes 32
  308.3 1.4 dynamic-update-slice.12
  310.3 1.4 dynamic-update-slice.7
  311.7 9.9 %all-reduce.18 = (f32[2]{0:T(128)S(1)}, f32[2]{0:T(128)S(1)}) all-reduce(f32[2]{0:T(128)S(1)} %dynamic-update-slice.7, f32[2]{0:T(128)S(1)} %dynamic-update-slice.12), channel_id=1, replica_groups=mesh['rep_0'=4,'rep_1'=2,'rep_2'=2,'stripe_0'=4,'stripe_1'=4] {'rep_2'}, use_global_device_ids=true, to_apply=%add.7 | all-reduce | flops 4 | bytes 32
  322.2 1.4 dynamic-update-slice.13
  324.2 1.4 dynamic-update-slice.8
  325.6 6.1 %all-reduce.16 = (f32[4]{0:T(128)S(1)}, f32[4]{0:T(128)S(1)}) all-reduce(f32[4]{0:T(128)S(1)} %dynamic-update-slice.8, f32[4]{0:T(128)S(1)} %dynamic-update-slice.13), channel_id=1, replica_groups=mesh['rep_0'=4,'rep_1'=2,'rep_2'=2,'stripe_0'=4,'stripe_1'=4] {'stripe_0'}, use_global_device_ids=true, to_apply=%add.8 | all-reduce | flops 8 | bytes 64
  332.3 1.4 dynamic-update-slice.14
  334.3 1.4 dynamic-update-slice.9
  335.6 6.6 %all-reduce.15 = (f32[4]{0:T(128)S(1)}, f32[4]{0:T(128)S(1)}) all-reduce(f32[4]{0:T(128)S(1)} %dynamic-update-slice.9, f32[4]{0:T(128)S(1)} %dynamic-update-slice.14), channel_id=1, replica_groups=mesh['rep_0'=4,'rep_1'=2,'rep_2'=2,'stripe_0'=4,'stripe_1'=4] {'stripe_1'}, use_global_device_ids=true, to_apply=%add.9 | all-reduce | flops 8 | bytes 64
  345.8 107.2 %all-gather.3.cloned.1.call-done = f32[4096,512]{1,0:T(8,128)} async-done(((f32[256,512]{1,0:T(8,128)}), f32[4096,512]{1,0:T(8,128)}) %all-gather.3.cloned.1.call-update) | async-done | bytes 8388624 | tf_op jit(solution)/shard_map/all_gather | solution.py:99
  453.1 7.7 %gather_fusion.2 = f32[16,256,512]{2,1,0:T(8,128)} fusion(f32[16,256,512]{2,1,0:T(8,128)} %bitcast.61, s32[1024]{0:T(1024)S(1)} %pad_clamp_fusion), kind=kCustom, calls=%fused_computation.2 | custom fusion | bytes 16777280 | tf_op jit(solution)/shard_map/jit(_take)/gather | solution.py:105
  460.7 6.0 %bitcast_select_fusion = f32[4096,512]{1,0:T(8,128)} fusion(f32[16,256,512]{2,1,0:T(8,128)} %gather_fusion.2, pred[4096]{0:T(1024)(128)(4,1)S(1)} %broadcast_in_dim.40), kind=kLoop, calls=%fused_computation.3 | loop fusion | flops 2097152 | bytes 16781312 | tf_op jit(solution)/shard_map/jit(_take)/select_n | solution.py:105
  (76 shorter events, 16.2 us)
Async XLA Ops:
  7.2 11.4 %copy-start = (bf16[256,512]{1,0:T(8,128)(2,1)S(1)}, bf16[256,512]{1,0:T(8,128)(2,1)}, u32[]{:S(2)}) copy-start(bf16[256,512]{1,0:T(8,128)(2,1)} %param.5) | copy-start | bytes 786436
  7.2 169.2 %reduce-scatter.2.cloned.1.call-start = ((), (), s32[]{:S(2)}) async-start(), calls=%async_computation.1 | async-start | bytes 8912896 | tf_op jit(solution)/shard_map/reduce_scatter | solution.py:65
  34.1 143.4 %copy-start.8 = (u32[256]{0:T(256)S(1)}, u32[256]{0:T(256)}, u32[]{:S(2)}) copy-start(u32[256]{0:T(256)} %constant.146) | copy-start | bytes 3076
  34.2 418.9 %all-gather.3.cloned.1.call-start = ((), (), s32[]{:S(2)}) async-start(), calls=%async_computation.2 | async-start | bytes 8912896 | tf_op jit(solution)/shard_map/all_gather | solution.py:99
  176.3 12.9 %collective-permute-start = (f32[256,512]{0,1:T(8,128)}, f32[256,512]{0,1:T(8,128)S(1)}, u32[]{:S(2)}, u32[]{:S(2)}) collective-permute-start(f32[256,512]{0,1:T(8,128)} %reduce-scatter.2.cloned.1.call-done), channel_id=1, source_target_pairs={{0,128},{16,144},{32,160},{48,176},{64,192},{80,208},{96,224},{112... | collective-permute-start | bytes 1572872 | tf_op jit(solution)/shard_map/ppermute | solution.py:19
  189.3 1.6 copy-start.3
  191.2 6.9 %copy-start.7 = (u32[256]{0:T(256)S(1)}, u32[256]{0:T(256)}, u32[]{:S(2)}) copy-start(u32[256]{0:T(256)} %constant.151) | copy-start | bytes 3076
  191.2 15.4 %copy-start.6 = (u32[256]{0:T(256)S(1)}, u32[256]{0:T(256)}, u32[]{:S(2)}) copy-start(u32[256]{0:T(256)} %constant.156) | copy-start | bytes 3076
  191.2 25.7 %copy-start.5 = (u32[256]{0:T(256)S(1)}, u32[256]{0:T(256)}, u32[]{:S(2)}) copy-start(u32[256]{0:T(256)} %constant.161) | copy-start | bytes 3076
  191.2 37.4 %copy-start.4 = (u32[256]{0:T(256)S(1)}, u32[256]{0:T(256)}, u32[]{:S(2)}) copy-start(u32[256]{0:T(256)} %constant.166) | copy-start | bytes 3076
  196.7 54.3 %copy-start.1 = (f32[512,512]{1,0:T(8,128)}, f32[512,512]{1,0:T(8,128)S(1)}, u32[]{:S(2)}) copy-start(f32[512,512]{1,0:T(8,128)S(1)} %get-tuple-element.13) | copy-start | bytes 3145732
  253.0 1.9 copy-start.2
  261.9 22.3 %collective-permute-start.1 = (f32[512,512]{1,0:T(8,128)S(1)}, f32[512,512]{1,0:T(8,128)S(1)}, u32[]{:S(2)}, u32[]{:S(2)}) collective-permute-start(f32[512,512]{1,0:T(8,128)S(1)} %fusion.47), channel_id=1, source_target_pairs={{0,128},{16,144},{32,160},{48,176},{64,192},{80,208},{96,224},{112... | collective-permute-start | bytes 3145736 | tf_op jit(solution)/shard_map/ppermute | solution.py:19
Sparse Core Ops, SparseCore 0:
  34.3 142.0 reduce-scatter.1
  345.7 107.2 all-gather.2
